TPU v7x, 128 devices: a whole 4x4x4 slice. The times are simulated.
128 devices in a mesh: pair: 8 (over x, core), aux: 16 (over y, z).
Axes of the slice: x: 4, y: 4, z: 4, core: 2. Of those that a mesh axis runs over, the one named last changes fastest.
Arguments:
- left_active: bfloat16 [80, 128, 61440], P('pair', None, 'aux'), may hold values from -0.375 to 0.375
- right_active: bfloat16 [80, 128, 61440], P('pair', None, 'aux'), may hold values from -0.375 to 0.375
- amps_active: bfloat16 [80, 128, 128], P('pair', 'aux'), may hold values from -0.5 to 0.5
- rank_active: int32 [80], P('pair'), may hold values from 80 to 128, as said below
- gap_active: float32 [80], P('pair'), may hold values from 0.5 to 2
- energy_active: float32 [80, 128], P('pair'), may hold values from 0.5 to 4
- intersect_active: bfloat16 [80, 4, 128, 128], P('pair'), may hold values from -0.75 to 0.75
- fock_active: float32 [80, 4], P('pair'), may hold values from -2 to 2
- neighbor_active: int32 [80, 4], P('pair'), may hold values from 0 to 79
- left_env: bfloat16 [32, 48, 61440], P('pair', None, 'aux'), may hold values from -0.375 to 0.375
- right_env: bfloat16 [32, 48, 61440], P('pair', None, 'aux'), may hold values from -0.375 to 0.375
- amps_env: bfloat16 [32, 48, 48], P('pair', 'aux'), may hold values from -0.875 to 0.875
- rank_env: int32 [32], P('pair'), may hold values from 24 to 48, as said below
- gap_env: float32 [32], P('pair'), may hold values from 0.5 to 2
- energy_env: float32 [32, 48], P('pair'), may hold values from 0.5 to 4
- intersect_env: bfloat16 [32, 4, 48, 48], P('pair'), may hold values from -1.25 to 1.25
- fock_env: float32 [32, 4], P('pair'), may hold values from -2 to 2
- neighbor_env: int32 [32, 4], P('pair'), may hold values from 0 to 31
Outputs:
- new_active: float32 [80, 128, 128], P('pair', 'aux')
- new_env: float32 [32, 48, 48], P('pair', 'aux')
Inputs may be any that keep to these rules, and one draw needn't show every extreme that they name: `rank_active`: multiples of 8; the first active pair has rank 128. `rank_env`: multiples of 8; the first environment pair has rank 48.
All inputs are finite; a program needn't handle non-finite values.
Results may differ from a plain program's by a relative error of at most 0.0041.
Values may be sent and summed in bfloat16 or wider, within the bound.
A program may use at most 128 MiB of HBM per device.

v0:
```python
import jax
import jax.numpy as jnp
from jax import lax
from jax.sharding import Mesh
from jax.sharding import PartitionSpec as P

AUX = ("aux_0", "aux_1")


HIGHEST = lax.Precision.HIGHEST


def whole_of(shard, axes, dim):
    result = shard
    for number in range(len(axes) - 1, -1, -1):
        result = lax.all_gather(result, axes[number], axis=dim, tiled=True)
    return result


def joined_along(tiles, dim):
    tiles = jnp.moveaxis(tiles, 0, dim)
    lengths = tiles.shape
    return tiles.reshape(*lengths[:dim], lengths[dim] * lengths[dim + 1], *lengths[dim + 2 :])


def gather_packed(arrays, axis, dims):
    flat = jnp.concatenate([a.reshape(-1) for a in arrays])
    lines, at, gathered = (lax.all_gather(flat, axis), 0, [])
    for a, dim in zip(arrays, dims):
        tiles = lines[:, at : at + a.size].reshape(-1, *a.shape)
        gathered.append(joined_along(tiles, dim))
        at += a.size
    return tuple(gathered)


def split_up(shard, dim, size):
    lengths = shard.shape
    tiles = shard.reshape(*lengths[:dim], size, lengths[dim] // size, *lengths[dim + 1 :])
    return jnp.moveaxis(tiles, dim, 0)


def sum_at_owner(shard, axis, dim):
    size = lax.axis_size(axis)
    tiles = lax.all_to_all(split_up(shard, dim, size), axis, 0, 0, tiled=True)
    return jnp.sum(tiles.astype(jnp.float32), axis=0)


def shard_mask(pair_ranks, row_count, full_width, row_start):
    row_index = row_start + jnp.arange(row_count, dtype=jnp.int32)
    col_index = jnp.arange(full_width, dtype=jnp.int32)
    return (row_index[None, :, None] < pair_ranks[:, None, None]) & (
        col_index[None, None, :] < pair_ranks[:, None, None]
    )


def aux_terms(left_ints, right_ints, own_full, with_ladder):
    summed_terms = jnp.einsum(
        "paq,pbq->pab", left_ints, right_ints, preferred_element_type=jnp.float32
    )
    if with_ladder:
        cross_left = jnp.einsum(
            "pab,paq->pbq", own_full, left_ints, preferred_element_type=jnp.float32
        ).astype(jnp.bfloat16)
        cross_right = jnp.einsum(
            "pab,pbq->paq", own_full, right_ints, preferred_element_type=jnp.float32
        ).astype(jnp.bfloat16)
        summed_terms = summed_terms + jnp.einsum(
            "pcq,pbq->pcb", cross_left, right_ints, preferred_element_type=jnp.float32
        )
        summed_terms = summed_terms + jnp.einsum(
            "pcq,paq->pca", cross_left, cross_right, preferred_element_type=jnp.float32
        )
    return summed_terms


def couple_blocks(cols_over, near_block, intersect, fock_weights):
    right_part = jnp.einsum(
        "pkst,pkut->pksu", near_block, intersect, preferred_element_type=jnp.float32
    )
    right_part = right_part * fock_weights[:, :, None, None]
    return jnp.einsum(
        "pkrs,pksu->pru", cols_over.astype(jnp.float32), right_part, precision=HIGHEST
    )


def finish(summed, amp_shard, pair_ranks, pair_gaps, energy, row_start):
    row_count = amp_shard.shape[1]
    inside = shard_mask(pair_ranks, row_count, amp_shard.shape[2], row_start)
    energy_rows = lax.dynamic_slice_in_dim(energy, row_start, row_count, 1)
    denominator = energy_rows[:, :, None] + energy[:, None, :] + pair_gaps[:, None, None]
    return jnp.where(inside, amp_shard.astype(jnp.float32) - summed / denominator, jnp.float32(0.0))


def shards(
    left_active,
    right_active,
    amps_active,
    rank_active,
    gap_active,
    energy_active,
    intersect_active,
    fock_active,
    neighbor_active,
    left_env,
    right_env,
    amps_env,
    rank_env,
    gap_env,
    energy_env,
    intersect_env,
    fock_env,
    neighbor_env,
):
    aux_place = lax.axis_index(AUX)
    rows_act = amps_active.shape[1]
    rows_env = amps_env.shape[1]
    start_act = aux_place * rows_act
    start_env = aux_place * rows_env
    shard_act = jnp.where(
        shard_mask(rank_active, rows_act, amps_active.shape[2], start_act),
        amps_active,
        jnp.zeros_like(amps_active),
    )
    shard_env = jnp.where(
        shard_mask(rank_env, rows_env, amps_env.shape[2], start_env),
        amps_env,
        jnp.zeros_like(amps_env),
    )
    own_act = whole_of(shard_act, AUX, 1)
    block_act, block_env = gather_packed((shard_act, shard_env), "pair", (0, 0))
    cols_over_act = lax.dynamic_slice_in_dim(intersect_active, start_act, rows_act, 3)
    cols_over_env = lax.dynamic_slice_in_dim(intersect_env, start_env, rows_env, 3)
    terms_act = aux_terms(left_active, right_active, own_act, True) + couple_blocks(
        cols_over_act, block_act[neighbor_active], intersect_active, fock_active
    )
    terms_env = aux_terms(left_env, right_env, None, False) + couple_blocks(
        cols_over_env, block_env[neighbor_env], intersect_env, fock_env
    )
    summed_act, summed_env = (
        sum_at_owner(terms_act.astype(jnp.bfloat16), AUX, 1),
        sum_at_owner(terms_env.astype(jnp.bfloat16), AUX, 1),
    )
    new_active = finish(summed_act, shard_act, rank_active, gap_active, energy_active, start_act)
    new_env = finish(summed_env, shard_env, rank_env, gap_env, energy_env, start_env)
    return (new_active, new_env)


def solution(mesh):
    finer = Mesh(mesh.devices.reshape(mesh.shape["pair"], 4, 4), ("pair", "aux_0", "aux_1"))
    return jax.shard_map(
        shards,
        mesh=finer,
        in_specs=(
            P("pair", None, AUX),
            P("pair", None, AUX),
            P("pair", AUX, None),
            P("pair"),
            P("pair"),
            P("pair", None),
            P("pair", None, None, None),
            P("pair", None),
            P("pair", None),
            P("pair", None, AUX),
            P("pair", None, AUX),
            P("pair", AUX, None),
            P("pair"),
            P("pair"),
            P("pair", None),
            P("pair", None, None, None),
            P("pair", None),
            P("pair", None),
        ),
        out_specs=(P("pair", AUX, None), P("pair", AUX, None)),
        check_vma=False,
    )
```

profile of v0, /device:TPU:0, one launch (start us, length us, event | category | flops | bytes accessed | tf_op | source)
XLA Modules:
  0.0 121.1 jit_solution(1759668718932934217)
XLA Ops:
  7.2 0.0 all-reduce.3.cloned.1.call-start
  7.2 0.8 iota_compare_fusion
  8.1 0.7 broadcast_compare_fusion
  8.8 0.7 iota_compare_fusion.1
  9.5 0.7 broadcast_compare_fusion.1
  10.3 0.8 and_select_fusion.3
  11.0 0.1 reshape.139
  11.1 0.8 fusion.42
  11.9 1.2 %dynamic-slice = u32[1]{0:T(128)} dynamic-slice(u32[128]{0:T(128)} %constant.50, u32[]{:T(128)S(6)} %add.122), dynamic_slice_sizes={1} | dynamic-slice | bytes 12
  13.9 0.5 dynamic-update-slice
  14.4 0.7 copy-done.2
  15.0 0.0 all-reduce.3.cloned.1.call-update
  15.1 0.8 and_select_fusion.1
  15.9 12.2 %all_gather.12 = bf16[10,32,128]{2,1,0:T(8,128)(2,1)S(1)} all-gather(bf16[10,8,128]{2,1,0:T(8,128)(2,1)S(1)} %and_select_fusion.1), channel_id=1, replica_groups=mesh['pair'=8,'aux_0'=4,'aux_1'=4] {'aux_1'}, dimensions={1}, use_global_device_ids=true | all-gather | bytes 102400 | tf_op jit(solution)/shard_map/all_gather | solution.py:16
  28.0 13.1 %all_gather.13 = bf16[10,128,128]{2,1,0:T(8,128)(2,1)S(1)} all-gather(bf16[10,32,128]{2,1,0:T(8,128)(2,1)S(1)} %all_gather.12), channel_id=1, replica_groups=mesh['pair'=8,'aux_0'=4,'aux_1'=4] {'aux_0'}, dimensions={1}, use_global_device_ids=true | all-gather | bytes 409600 | tf_op jit(solution)/shard_map/all_gather | solution.py:16
  41.2 10.4 %convolution_convert_fusion = bf16[10,128,3840]{2,1,0:T(8,128)(2,1)} fusion(bf16[10,128,128]{2,1,0:T(8,128)(2,1)S(1)} %all_gather.13, bf16[10,128,3840]{2,1,0:T(8,128)(2,1)} %param.18), kind=kOutput, calls=%fused_computation.4 | convolution fusion | flops 1263206400 | bytes 19988480 | tf_op jit(solution)/shard_map/pab,paq->pbq/dot_general | solution.py:61
  51.5 9.3 %fusion.24 = f32[10,128,128]{2,1,0:T(8,128)S(1)} fusion(bf16[10,128,3840]{2,1,0:T(8,128)(2,1)} %param.18, bf16[10,128,3840]{2,1,0:T(8,128)(2,1)} %param.19), kind=kOutput, calls=%fused_computation.42 | convolution fusion | flops 1258291200 | bytes 20316160 | tf_op jit(solution)/shard_map/paq,pbq->pab/dot_general | solution.py:57
  60.9 10.2 %convolution_add_fusion = f32[10,128,128]{2,1,0:T(8,128)} fusion(f32[10,128,128]{2,1,0:T(8,128)S(1)} %fusion.24, bf16[10,128,3840]{2,1,0:T(8,128)(2,1)} %convolution_convert_fusion, bf16[10,128,3840]{2,1,0:T(8,128)(2,1)} %param.19), kind=kOutput, calls=%fused_computation.11 | convolution fusion | flops 1258455040 | bytes 20971520 | tf_op jit(solution)/shard_map/pcq,pbq->pcb/dot_general | solution.py:67
  71.1 10.4 %fusion.6 = f32[10,128,128]{2,1,0:T(8,128)} fusion(f32[10,128,128]{2,1,0:T(8,128)} %convolution_add_fusion, bf16[10,128,3840]{2,1,0:T(8,128)(2,1)} %convolution_convert_fusion, bf16[10,128,128]{2,1,0:T(8,128)(2,1)S(1)} %all_gather.13, bf16[10,128,3840]{2,1,0:T(8,128)(2,1)} %param.19), kind=kOutput, calls=%fused_computation.8 | convolution fusion | flops 2521661440 | bytes 21299200 | tf_op jit(solution)/shard_map/pcq,paq->pca/dot_general | solution.py:70
  81.5 0.1 copy.34
  81.6 0.1 reshape.144
  81.7 0.1 copy.35
  81.8 0.1 reshape.152
  81.9 0.1 constant_dynamic-slice_fusion.1
  82.1 0.2 copy.44
  82.2 0.1 constant_dynamic-slice_fusion
  82.3 0.1 copy.40
  82.4 0.1 constant_dynamic-slice_fusion.2
  82.5 1.1 reshape.158
  83.6 0.1 reshape_reshape.6
  83.7 0.1 reshape_reshape.7
  83.8 0.6 gather_fusion.1
  84.4 0.2 convolution_multiply_fusion.1
  84.6 0.3 convolution_bitcast_fusion
  84.9 1.9 %fusion.21 = bf16[4,48,48]{2,1,0:T(8,128)(2,1)S(1)} fusion(f32[4,48,48]{2,1,0:T(8,128)S(1)} %convolution_bitcast_fusion, bf16[4,48,3840]{2,1,0:T(8,128)(2,1)S(1)} %copy-done, bf16[4,48,3840]{2,1,0:T(8,128)(2,1)} %param.28), kind=kOutput, calls=%fused_computation.17 | convolution fusion | flops 70797312 | bytes 3004416 | tf_op jit(solution)/shard_map/paq,pbq->pab/dot_general | solution.py:57
  86.8 0.7 reshape.170
  87.6 5.5 %all-to-all-start.1 = ((bf16[16,2,288]{2,1,0:T(2,128)(2,1)}), bf16[16,2,288]{2,1,0:T(2,128)(2,1)S(1)}, u32[]{:S(2)}, u32[]{:S(2)}) async-start(bf16[16,2,288]{2,1,0:T(2,128)(2,1)} %reshape.170), calls=%async_computation.1 | async-start | bytes 49152 | tf_op jit(solution)/shard_map/all_to_all | solution.py:44
  93.1 0.6 gather_fusion
  93.7 0.8 convolution_multiply_fusion
  94.4 2.2 %fusion.18 = bf16[10,16,8,128]{3,2,1,0:T(8,128)(2,1)S(1)} fusion(f32[10,128,128]{2,1,0:T(8,128)} %fusion.6, f32[10,4,8,128]{3,2,1,0:T(8,128)S(1)} %convolution_multiply_fusion, bf16[10,4,128,128]{3,2,1,0:T(8,128)(2,1)S(1)} %copy-done.1, s32[]{:T(128)S(6)} %select_n.31), kind=kOutput, calls=%fused_computation.13 | convolution fusion | flops 63242240 | bytes 2457604 | tf_op jit(solution)/shard_map/pkrs,pksu->pru/dot_general | solution.py:81
  96.7 0.8 copy.48
  97.4 3.2 %all-to-all-done.1 = bf16[16,2,288]{2,1,0:T(2,128)(2,1)S(1)} async-done(((bf16[16,2,288]{2,1,0:T(2,128)(2,1)}), bf16[16,2,288]{2,1,0:T(2,128)(2,1)S(1)}, u32[]{:S(2)}, u32[]{:S(2)}) %all-to-all-start.1) | async-done | bytes 18464 | tf_op jit(solution)/shard_map/all_to_all | solution.py:44
  100.7 4.0 %all-to-all-start = ((bf16[16,10,8,128]{3,2,1,0:T(8,128)(2,1)}), bf16[16,10,8,128]{3,2,1,0:T(8,128)(2,1)S(1)}, u32[]{:S(2)}, u32[]{:S(2)}) async-start(bf16[16,10,8,128]{3,2,1,0:T(8,128)(2,1)} %bitcast.44), calls=%async_computation | async-start | bytes 655360 | tf_op jit(solution)/shard_map/all_to_all | solution.py:44
  104.7 0.1 reshape.171
  104.8 0.7 and_select_fusion.2
  105.5 8.0 %all-to-all-done = bf16[16,10,8,128]{3,2,1,0:T(8,128)(2,1)S(1)} async-done(((bf16[16,10,8,128]{3,2,1,0:T(8,128)(2,1)}), bf16[16,10,8,128]{3,2,1,0:T(8,128)(2,1)S(1)}, u32[]{:S(2)}, u32[]{:S(2)}) %all-to-all-start) | async-done | bytes 327712 | tf_op jit(solution)/shard_map/all_to_all | solution.py:44
  113.5 0.1 convert_reduce_fusion
  113.6 0.7 and_select_fusion
  (41 shorter events, 0.2 us)
Async XLA Ops:
  7.2 77.7 %copy-start = (bf16[4,48,3840]{2,1,0:T(8,128)(2,1)S(1)}, bf16[4,48,3840]{2,1,0:T(8,128)(2,1)}, u32[]{:S(2)}) copy-start(bf16[4,48,3840]{2,1,0:T(8,128)(2,1)} %param.27) | copy-start | bytes 4423684
  7.2 75.3 %all-reduce.3.cloned.1.call-start = ((), (), s32[]{:S(2)}) async-start(), calls=%async_computation.2 | async-start | bytes 348160
  14.4 0.7 copy-start.2
  71.1 10.4 %copy-start.9 = (s32[10,4]{0,1:T(4,128)S(1)}, s32[10,4]{0,1:T(4,128)}, u32[]{:S(2)}) copy-start(s32[10,4]{0,1:T(4,128)} %param.26) | copy-start | bytes 484
  71.1 10.7 %copy-start.8 = (f32[10,4]{0,1:T(4,128)S(1)}, f32[10,4]{0,1:T(4,128)}, u32[]{:S(2)}) copy-start(f32[10,4]{0,1:T(4,128)} %param.25) | copy-start | bytes 484
  71.1 10.8 %copy-start.10 = (s32[4,4]{1,0:T(4,128)S(1)}, s32[4,4]{1,0:T(4,128)}, u32[]{:S(2)}) copy-start(s32[4,4]{1,0:T(4,128)} %param.35) | copy-start | bytes 196
  71.1 10.9 %copy-start.3 = (bf16[4,4,48,48]{3,2,1,0:T(8,128)(2,1)S(1)}, bf16[4,4,48,48]{3,2,1,0:T(8,128)(2,1)}, u32[]{:S(2)}) copy-start(bf16[4,4,48,48]{3,2,1,0:T(8,128)(2,1)} %param.33) | copy-start | bytes 221188
  71.1 11.1 %copy-start.7 = (f32[4,48]{1,0:T(4,128)S(1)}, f32[4,48]{1,0:T(4,128)}, u32[]{:S(2)}) copy-start(f32[4,48]{1,0:T(4,128)} %param.32) | copy-start | bytes 2308
  71.1 11.3 %copy-start.5 = (f32[10,128]{1,0:T(8,128)S(1)}, f32[10,128]{1,0:T(8,128)}, u32[]{:S(2)}) copy-start(f32[10,128]{1,0:T(8,128)} %param.23) | copy-start | bytes 15364
  71.1 13.3 %copy-start.13 = (f32[4,4]{1,0:T(4,128)S(1)}, f32[4,4]{1,0:T(4,128)}, u32[]{:S(2)}) copy-start(f32[4,4]{1,0:T(4,128)} %param.34) | copy-start | bytes 196
  71.1 22.5 %copy-start.1 = (bf16[10,4,128,128]{3,2,1,0:T(8,128)(2,1)S(1)}, bf16[10,4,128,128]{3,2,1,0:T(8,128)(2,1)}, u32[]{:S(2)}) copy-start(bf16[10,4,128,128]{3,2,1,0:T(8,128)(2,1)} %param.24) | copy-start | bytes 3932164
  81.5 23.3 %copy-start.6 = (bf16[4,3,48]{2,0,1:T(4,128)(2,1)S(1)}, bf16[4,3,48]{2,0,1:T(4,128)(2,1)}, u32[]{:S(2)}) copy-start(bf16[4,3,48]{2,0,1:T(4,128)(2,1)} %param.29) | copy-start | bytes 3460
  81.5 23.3 %copy-start.12 = (f32[4]{0:T(128)S(1)}, f32[4]{0:T(128)}, u32[]{:S(2)}) copy-start(f32[4]{0:T(128)} %param.31) | copy-start | bytes 52
  81.5 32.0 %copy-start.4 = (bf16[10,8,128]{2,1,0:T(8,128)(2,1)S(1)}, bf16[10,8,128]{2,1,0:T(8,128)(2,1)}, u32[]{:S(2)}) copy-start(bf16[10,8,128]{2,1,0:T(8,128)(2,1)} %param.20) | copy-start | bytes 61444
  81.5 32.0 %copy-start.11 = (f32[10]{0:T(128)S(1)}, f32[10]{0:T(128)}, u32[]{:S(2)}) copy-start(f32[10]{0:T(128)} %param.22) | copy-start | bytes 124
  87.6 13.1 %all-to-all-start.1 = ((bf16[16,2,288]{2,1,0:T(2,128)(2,1)}), bf16[16,2,288]{2,1,0:T(2,128)(2,1)S(1)}, u32[]{:S(2)}, u32[]{:S(2)}) async-start(bf16[16,2,288]{2,1,0:T(2,128)(2,1)} %reshape.170), calls=%async_computation.1 | async-start | bytes 49152 | tf_op jit(solution)/shard_map/all_to_all | solution.py:44
  100.7 12.8 %all-to-all-start = ((bf16[16,10,8,128]{3,2,1,0:T(8,128)(2,1)}), bf16[16,10,8,128]{3,2,1,0:T(8,128)(2,1)S(1)}, u32[]{:S(2)}, u32[]{:S(2)}) async-start(bf16[16,10,8,128]{3,2,1,0:T(8,128)(2,1)} %bitcast.44), calls=%async_computation | async-start | bytes 655360 | tf_op jit(solution)/shard_map/all_to_all | solution.py:44
Sparse Core Ops, SparseCore 0:
  15.2 62.6 all-reduce.2
where the time goes:
time: 122 us; the launch traced here: 121 us
  matrix products  45.6 us (37%)
  blocking collectives  25.3 us (21%)
  between operations  15 us (12%)
  waiting for transfers between devices  11.2 us (9%)
  starting transfers between devices  9.5 us (8%)
  local copies, waits for them, and re-layouts  7.61 us (6%)
  other arithmetic  6.92 us (6%)
    all_gather x2, blocking collectives, whole_of(): result = lax.all_gather(result, axes[number], axis=dim, tiled=True)  25.3 us
    dot_general x2, matrix products, aux_terms(): jnp.einsum('paq,pbq->pab', left_ints, right_ints, preferred_element_type=...  11.2 us
    all_to_all x2, waiting for transfers between devices, sum_at_owner(): tiles = lax.all_to_all(split_up(shard, dim, size), axis, 0, 0, tiled=True)  11.2 us
    dot_general x1, matrix products, aux_terms(): jnp.einsum('pcq,paq->pca', cross_left, cross_right, preferred_element_typ...  10.4 us
    dot_general x1, matrix products, aux_terms(): jnp.einsum('pab,paq->pbq', own_full, left_ints, preferred_element_type=jn...  10.4 us
    dot_general x1, matrix products, aux_terms(): jnp.einsum('pcq,pbq->pcb', cross_left, right_ints, preferred_element_type...  10.2 us
    all_to_all x2, starting transfers between devices, sum_at_owner(): tiles = lax.all_to_all(split_up(shard, dim, size), axis, 0, 0, tiled=True)  9.46 us
    unnamed x35, local copies, waits for them, and re-layouts  3.61 us
  transfers between devices with their start and end apart: 3, of which 2 were waited for; matrix products, arithmetic and copies ran while one was open for 39% of the time, Pallas kernels for 0%

commit v1 on v0

v1 whole, which is shorter than its diff:
```python
import functools

import jax
import jax.numpy as jnp
from jax import lax
from jax.experimental import pallas as pl
from jax.experimental.pallas import tpu as pltpu
from jax.sharding import PartitionSpec as P

MESH = pl.DeviceIdType.MESH
F32 = jnp.float32
BF16 = jnp.bfloat16
NT = (((1,), (1,)), ((), ()))
TN = (((0,), (0,)), ((), ()))
AHEAD = 3


def iota(shape, dim):
    return lax.broadcasted_iota(jnp.int32, shape, dim)


def nt(a, b):
    return lax.dot_general(a, b, NT, preferred_element_type=F32)


def mm(a, b):
    return jnp.dot(a, b, preferred_element_type=F32)


def kernel(
    n_aux,
    n_pair,
    rank_a,
    gap_a,
    fock_a,
    near_a,
    rank_e,
    gap_e,
    fock_e,
    near_e,
    amps_a,
    amps_e,
    energy_a,
    energy_e,
    left_a,
    right_a,
    over_a,
    left_e,
    right_e,
    over_e,
    out_a,
    out_e,
    lbuf,
    rbuf,
    lebuf,
    rebuf,
    obuf,
    oebuf,
    wbuf,
    webuf,
    own_a,
    own_e,
    tall,
    near_rows_a,
    near_rows_e,
    part,
    got,
    l_sem,
    r_sem,
    le_sem,
    re_sem,
    o_sem,
    tsend,
    trecv,
    pasend,
    parecv,
    pesend,
    perecv,
    ssend,
    srecv,
):
    pairs = left_a.shape[0]
    envs = left_e.shape[0]
    nb = over_a.shape[1]
    re_ = left_e.shape[1]
    rows_e = amps_e.shape[0]
    me = lax.axis_index("pair")
    j = lax.axis_index("aux")

    def load_pair(p):
        return (
            pltpu.make_async_copy(left_a.at[p], lbuf.at[p], l_sem.at[p]),
            pltpu.make_async_copy(right_a.at[p], rbuf.at[p], r_sem.at[p]),
        )

    def start_pair(p):
        for copy in load_pair(p):
            copy.start()

    def load_env(q):
        c, i = q // 2, q % 2
        return (
            pltpu.make_async_copy(left_e.at[q], lebuf.at[c, pl.ds(i * re_, re_)], le_sem.at[q]),
            pltpu.make_async_copy(right_e.at[q], rebuf.at[c, pl.ds(i * 64, re_)], re_sem.at[q]),
        )

    over_copies = (
        pltpu.make_async_copy(over_a, obuf, o_sem.at[0]),
        pltpu.make_async_copy(over_e, oebuf, o_sem.at[1]),
    )
    for p in range(AHEAD):
        start_pair(p)
    for copy in over_copies:
        copy.start()

    barrier = pltpu.get_barrier_semaphore()

    @pl.loop(1, n_aux)
    def _(o):
        pl.semaphore_signal(barrier, inc=1, device_id={"aux": lax.rem(j + o, n_aux)}, device_id_type=MESH)

    @pl.loop(1, n_pair)
    def _(o):
        pl.semaphore_signal(barrier, inc=1, device_id={"pair": lax.rem(me + o, n_pair)}, device_id_type=MESH)

    lanes8 = iota((8, 128), 1)
    subs8 = iota((8, 128), 0)
    for p in range(pairs):
        rank = rank_a[p]
        inside = (subs8 + 8 * j < rank) & (lanes8 < rank)
        own_a[p] = jnp.where(inside, amps_a[p].astype(F32), 0.0).astype(BF16)
    for q in range(envs):
        rank = rank_e[q]
        slab = jnp.zeros((8, 128), F32)
        for r in range(rows_e):
            line = jnp.pad(amps_e[r].astype(F32)[q : q + 1], ((0, 0), (0, 128 - re_)))
            slab = jnp.where(subs8 == r, line, slab)
        inside = (subs8 + rows_e * j < rank) & (lanes8 < rank) & (subs8 < rows_e)
        own_e[q] = jnp.where(inside, slab, 0.0).astype(BF16)
    tall[j] = own_a[...]
    near_rows_a[pl.ds(me * pairs, pairs)] = own_a[...]
    near_rows_e[pl.ds(me * envs, envs)] = own_e[...]

    pl.semaphore_wait(barrier, n_aux - 1 + n_pair - 1)

    def send_t(o):
        return pltpu.make_async_remote_copy(
            own_a, tall.at[j], tsend.at[o], trecv.at[o],
            device_id={"aux": lax.rem(j + o, n_aux)}, device_id_type=MESH,
        )

    def send_pa(o):
        return pltpu.make_async_remote_copy(
            own_a, near_rows_a.at[pl.ds(me * pairs, pairs)], pasend.at[o], parecv.at[o],
            device_id={"pair": lax.rem(me + o, n_pair)}, device_id_type=MESH,
        )

    def send_pe(o):
        return pltpu.make_async_remote_copy(
            own_e, near_rows_e.at[pl.ds(me * envs, envs)], pesend.at[o], perecv.at[o],
            device_id={"pair": lax.rem(me + o, n_pair)}, device_id_type=MESH,
        )

    @pl.loop(1, n_aux)
    def _(o):
        send_t(o).start()

    @pl.loop(1, n_pair)
    def _(o):
        send_pa(o).start()
        send_pe(o).start()

    @pl.loop(0, pairs // 2)
    def _(h):
        for i in range(2):
            p = 2 * h + i

            @pl.when(p + AHEAD < pairs)
            def _():
                start_pair(p + AHEAD)

            if i == 1:

                @pl.when(h == pairs // 2 - 2)
                def _():
                    for q in range(envs):
                        for copy in load_env(q):
                            copy.start()

        for i in range(2):
            for copy in load_pair(2 * h + i):
                copy.wait()
        for i in range(2):
            wbuf[2 * h + i] = nt(lbuf[2 * h + i], rbuf[2 * h + i])

    lanes48 = iota((re_, 128), 1)
    for q in range(envs):
        for copy in load_env(q):
            copy.wait()
    for c in range(envs // 2):
        both = nt(lebuf[c], rebuf[c])
        webuf[c] = jnp.where(lanes48 < 64, both[:re_], both[re_:])

    for copy in over_copies:
        copy.wait()

    @pl.loop(1, n_pair)
    def _(o):
        send_pa(o).wait()
        send_pe(o).wait()

    @pl.loop(1, n_aux)
    def _(o):
        send_t(o).wait()

    pick_a = (lanes8 == subs8 + 8 * j).astype(F32)
    pick_e = ((lanes8 == subs8 + rows_e * j) & (subs8 < rows_e)).astype(F32)
    blank = jnp.zeros((8, 128), F32)

    def coupling(over, rows, pick, focks):
        total = None
        for k in range(nb):
            blocks = [blank] * 16
            blocks[k] = rows[k]
            blocks[4 + k] = rows[k]
            blocks[8 + k] = pick
            blocks[12 + k] = pick
            side = jnp.concatenate(blocks, axis=0).astype(BF16)
            term = nt(over[k], side[:, : over[k].shape[1]])
            total = term if total is None else total + term
        lane = iota(total.shape, 1)
        weight = jnp.zeros(total.shape, F32)
        for k in range(nb):
            weight = jnp.where((lane // 8) % 4 == k, focks[k], weight)
        scaled = total * weight
        high = scaled.astype(BF16).astype(F32)
        split = jnp.where(lane < 32, high, jnp.where(lane < 64, scaled - high, 0.0)).astype(BF16)
        cols = pltpu.roll(total, 64, 1).astype(BF16)
        return cols, split

    @pl.loop(0, pairs // 2)
    def _(h):
        for i in range(2):
            p = 2 * h + i
            t = tall[:, p].astype(F32).reshape(128, 128).astype(BF16)
            w = wbuf[p]
            v = lax.dot_general(t, w.astype(BF16), TN, preferred_element_type=F32)
            x = nt(v.astype(BF16), t)
            rows = [near_rows_a[near_a[k, p]].astype(F32) for k in range(nb)]
            cols, split = coupling([obuf[p, k] for k in range(nb)], rows, pick_a, [fock_a[k, p] for k in range(nb)])
            whole = w + v + x + nt(cols, split)
            part[:, p] = whole.reshape(n_aux, 8, 128).astype(BF16)

    place = iota((128, re_), 0)
    line = iota((128, re_), 1)
    packed = None
    for c in range(envs // 2):
        pieces = []
        sides = []
        for i in range(2):
            q = 2 * c + i
            rows = [near_rows_e[near_e[q, k]].astype(F32) for k in range(nb)]
            cols, split = coupling([oebuf[q, k] for k in range(nb)], rows, pick_e, [fock_e[q, k] for k in range(nb)])
            pieces.append(cols)
            sides.append(split.astype(F32))
        gap = jnp.zeros((64 - re_, 128), F32)
        side = jnp.concatenate([sides[0], gap, sides[1], gap], axis=0).astype(BF16)
        couple = jnp.where(lanes48 < 64, nt(pieces[0], side), nt(pieces[1], side))
        whole = jnp.where((lanes48 % 64) < re_, webuf[c] + couple, 0.0).astype(BF16)
        perm = (place % 8 >= rows_e * c) & (place % 8 < rows_e * (c + 1)) & (
            line == rows_e * (place // 8) + place % 8 - rows_e * c
        )
        moved = mm(perm.astype(F32).astype(BF16), whole)
        packed = moved if packed is None else packed + moved
    part[:, pairs] = packed.reshape(n_aux, 8, 128).astype(BF16)

    def send_s(o):
        d = lax.rem(j + o, n_aux)
        return pltpu.make_async_remote_copy(
            part.at[d], got.at[j], ssend.at[o], srecv.at[o],
            device_id={"aux": d}, device_id_type=MESH,
        )

    @pl.loop(1, n_aux)
    def _(o):
        send_s(o).start()

    got[j] = part[j]

    @pl.loop(1, n_aux)
    def _(o):
        send_s(o).wait()

    for p in range(pairs):
        total = got[0, p].astype(F32)
        for d in range(1, n_aux):
            total = total + got[d, p].astype(F32)
        rank = rank_a[p]
        inside = (subs8 + 8 * j < rank) & (lanes8 < rank)
        across = energy_a[pl.ds(p, 1), :]
        down = jnp.sum(jnp.where(lanes8 == subs8 + 8 * j, across, 0.0), axis=1, keepdims=True)
        out_a[p] = jnp.where(inside, own_a[p].astype(F32) - total / (down + across + gap_a[p]), 0.0)

    total = got[0, pairs].astype(F32)
    for d in range(1, n_aux):
        total = total + got[d, pairs].astype(F32)
    for q in range(envs):
        c, i = q // 2, q % 2
        mine = pltpu.roll(total, 64, 1) if i else total
        if c:
            mine = pltpu.roll(mine, 8 - rows_e, 0)
        rank = rank_e[q]
        inside = (subs8 + rows_e * j < rank) & (lanes8 < rank) & (subs8 < rows_e)
        across = jnp.pad(energy_e[pl.ds(q, 1), :], ((0, 0), (0, 128 - re_)))
        down = jnp.sum(jnp.where(lanes8 == subs8 + rows_e * j, across, 0.0), axis=1, keepdims=True)
        new = jnp.where(inside, own_e[q].astype(F32) - mine / (down + across + gap_e[q]), 0.0)
        for r in range(rows_e):
            out_e[r, pl.ds(q, 1), :] = new[r : r + 1, :re_]


def shards(
    left_a, right_a, amps_a, rank_a, gap_a, energy_a, over_a, fock_a, near_a,
    left_e, right_e, amps_e, rank_e, gap_e, energy_e, over_e, fock_e, near_e,
):
    n_aux, n_pair = 16, 8
    pairs, full, depth = left_a.shape
    envs, re_, _ = left_e.shape
    rows_e = amps_e.shape[1]
    nb = over_a.shape[1]
    smem = pl.BlockSpec(memory_space=pltpu.SMEM)
    vmem = pl.BlockSpec(memory_space=pltpu.VMEM)
    hbm = pl.BlockSpec(memory_space=pltpu.HBM)
    dma = pltpu.SemaphoreType.DMA
    slots = pairs + 1
    new_a, new_e = pl.pallas_call(
        functools.partial(kernel, n_aux, n_pair),
        out_shape=(
            jax.ShapeDtypeStruct((pairs, 8, full), F32),
            jax.ShapeDtypeStruct((rows_e, envs, re_), F32),
        ),
        in_specs=[smem] * 8 + [vmem] * 4 + [hbm] * 6,
        out_specs=(vmem, vmem),
        scratch_shapes=[
            pltpu.VMEM((pairs, full, depth), BF16),
            pltpu.VMEM((pairs, full, depth), BF16),
            pltpu.VMEM((envs // 2, 2 * re_, depth), BF16),
            pltpu.VMEM((envs // 2, 128, depth), BF16),
            pltpu.VMEM((pairs, nb, full, full), BF16),
            pltpu.VMEM((envs, nb, re_, re_), BF16),
            pltpu.VMEM((pairs, full, full), F32),
            pltpu.VMEM((envs // 2, re_, 128), F32),
            pltpu.VMEM((pairs, 8, 128), BF16),
            pltpu.VMEM((envs, 8, 128), BF16),
            pltpu.VMEM((n_aux, pairs, 8, 128), BF16),
            pltpu.VMEM((n_pair * pairs, 8, 128), BF16),
            pltpu.VMEM((n_pair * envs, 8, 128), BF16),
            pltpu.VMEM((n_aux, slots, 8, 128), BF16),
            pltpu.VMEM((n_aux, slots, 8, 128), BF16),
            dma((pairs,)),
            dma((pairs,)),
            dma((envs,)),
            dma((envs,)),
            dma((2,)),
            dma((n_aux,)),
            dma((n_aux,)),
            dma((n_pair,)),
            dma((n_pair,)),
            dma((n_pair,)),
            dma((n_pair,)),
            dma((n_aux,)),
            dma((n_aux,)),
        ],
        compiler_params=pltpu.CompilerParams(
            collective_id=0, has_side_effects=True, vmem_limit_bytes=56 * 2**20
        ),
        name="update",
    )(
        rank_a, gap_a, fock_a.T, near_a.T, rank_e, gap_e, fock_e, near_e,
        amps_a, jnp.swapaxes(amps_e, 0, 1), energy_a, energy_e,
        left_a, right_a, over_a, left_e, right_e, over_e,
    )
    return new_a, jnp.swapaxes(new_e, 0, 1)


def solution(mesh):
    p = P
    return jax.shard_map(
        shards,
        mesh=mesh,
        in_specs=(
            p("pair", None, "aux"), p("pair", None, "aux"), p("pair", "aux", None), p("pair"), p("pair"),
            p("pair", None), p("pair", None, None, None), p("pair", None), p("pair", None),
            p("pair", None, "aux"), p("pair", None, "aux"), p("pair", "aux", None), p("pair"), p("pair"),
            p("pair", None), p("pair", None, None, None), p("pair", None), p("pair", None),
        ),
        out_specs=(p("pair", "aux", None), p("pair", "aux", None)),
        check_vma=False,
    )
```

time: 122 us -> 32.4 us (0.27)
  matrix products: 45.6 us -> 0 us
  Pallas kernels: 0 us -> 28.8 us
  blocking collectives: 25.3 us -> 0 us
  between operations: 15 us -> 0.65 us
  waiting for transfers between devices: 11.2 us -> 0 us
  starting transfers between devices: 9.5 us -> 0 us
  other arithmetic: 6.92 us -> 0 us
  local copies, waits for them, and re-layouts: 7.61 us -> 2.68 us
    dot_general x9 -> x0, matrix products: 45.6 us -> none  [the longest x2 11.2 us: aux_terms(): jnp.einsum('paq,pbq->pab', left_ints, right_ints, preferred_element_type=...]
    pallas_call x0 -> x1, Pallas kernels: none -> 28.8 us  [shards(): pl.pallas_call(functools.partial(kernel, n_aux, n_pair), out_shape=(jax.S...]
    all_gather x2 -> x0, blocking collectives: 25.3 us -> none  [whole_of(): result = lax.all_gather(result, axes[number], axis=dim, tiled=True)]
    all_to_all x2 -> x0, waiting for transfers between devices: 11.2 us -> none  [sum_at_owner(): tiles = lax.all_to_all(split_up(shard, dim, size), axis, 0, 0, tiled=True)]
    all_to_all x2 -> x0, starting transfers between devices: 9.46 us -> none  [sum_at_owner(): tiles = lax.all_to_all(split_up(shard, dim, size), axis, 0, 0, tiled=True)]
    lt x4 -> x0, other arithmetic: 3.01 us -> none  [the longest x2 1.56 us: shard_mask(): col_index[None, None, :] < pair_ranks[:, None, None]]
    select_n x6 -> x0, other arithmetic: 2.97 us -> none  [the longest x2 1.4 us: finish(): jnp.where(inside, amp_shard.astype(jnp.float32) - summed / denominator, j...]
    unnamed x35 -> x2, local copies, waits for them, and re-layouts: 3.61 us -> 2.68 us
  transfers between devices with their start and end apart: 3 -> 0, of which waited for: 2 -> 0; matrix products, arithmetic and copies ran while one was open for 39% -> 0% of each run, Pallas kernels for 0% -> 0%
where the time goes in v1:
time: 32.4 us; the launch traced here: 32.1 us
  Pallas kernels  28.8 us (89%)
  local copies, waits for them, and re-layouts  2.68 us (8%)
  between operations  0.65 us (2%)
    pallas_call x1, Pallas kernels, shards(): pl.pallas_call(functools.partial(kernel, n_aux, n_pair), out_shape=(jax.S...  28.8 us
    unnamed x2, local copies, waits for them, and re-layouts  2.68 us

profile of v1, /device:TPU:0, one launch (start us, length us, event | category | flops | bytes accessed | tf_op | source)
XLA Modules:
  0.0 32.1 jit_solution(4699152631659726133)
XLA Ops:
  0.6 28.8 %update.1 = (f32[10,8,128]{2,1,0:T(8,128)}, f32[3,4,48]{2,1,0:T(4,128)}) custom-call(s32[10]{0:T(128)} %rank_a.1, f32[10]{0:T(128)} %gap_a.1, f32[4,10]{1,0:T(4,128)} %bitcast.6, s32[4,10]{1,0:T(4,128)} %bitcast.7, s32[4]{0:T(128)} %rank_e.1, f32[4]{0:T(128)} %gap_e.1, f32[4,4]{1,0:T(4,128)} %fock_e.1, s32[4,4]{1,0:T(4,128)} %near_e.1, ...), custom_call_target="tpu_custom_call" | custom-call | tf_op jit(solution)/shard_map/update/pallas_call | solution.py:335
  29.5 1.4 %copy.22 = f32[10,8,128]{2,1,0:T(8,128)} copy(f32[10,8,128]{2,1,0:T(8,128)} %get-tuple-element.8) | data formatting | bytes 81920
  30.9 1.3 %copy.23 = f32[4,3,48]{2,0,1:T(4,128)} copy(f32[4,3,48]{2,0,1:T(4,128)} %bitcast.4) | data formatting | bytes 4608
